TPU v7x, 32 devices: a whole 2x2x4 slice. The times are simulated.
32 devices in a mesh: ga: 8 (over z, x), band: 4 (over y, core).
Axes of the slice: x: 2, y: 2, z: 4, core: 2. Of those that a mesh axis runs over, the one named last changes fastest.
Arguments:
- coeffs: bfloat16 [2, 512, 40960], P(None, ('ga', 'band')), may hold values from -6 to 6
- projectors: bfloat16 [1280, 2, 40960], P(None, None, 'ga'), may hold values from -0.01953125 to 0.01953125
- block_coupling: float32 [1280, 18], replicated, may hold values from -12 to 12
- atom_counts: int32 [160], replicated, may hold values from 4 to 18, as said below
- wave_counts: int32 [8], P('ga'), may hold values from 3840 to 5120
Outputs:
- applied: bfloat16 [2, 512, 40960], P(None, ('ga', 'band'))
- band_energy: float32 [512], P(('ga', 'band'))
- total_energy: float32 [], replicated
Inputs may be any that keep to these rules, and one draw needn't show every extreme that they name: `atom_counts`: each atom has 4, 8 or 18 projectors, the counts sum to 1280 and the largest is 18.
All inputs are finite; a program needn't handle non-finite values.
Results may differ from a plain program's by a relative error of at most 0.013.
Values may be sent and summed in bfloat16 or wider, within the bound.
A program may use at most 128 MiB of HBM per device.

v0:
```python
import math
import jax
import jax.numpy as jnp
from jax import lax
from jax.sharding import PartitionSpec as P


def block_tables(atom_counts, row_ids):
    atom_ends = jnp.cumsum(atom_counts)
    atom_starts = atom_ends - atom_counts
    inside = (atom_starts[None, :] <= row_ids[:, None]) & (atom_ends[None, :] > row_ids[:, None])
    block_first = jnp.sum(jnp.where(inside, atom_starts[None, :], 0), axis=1)
    block_length = jnp.sum(jnp.where(inside, atom_counts[None, :], 0), axis=1)
    return (block_first, block_length)


def coupling_matrix(block_first, block_length, coupling_rows, column_count):
    column_ids = lax.iota(jnp.int32, column_count)
    offsets = column_ids[None, :] - block_first[:, None]
    matrix = jnp.zeros((coupling_rows.shape[0], column_count), jnp.float32)
    for offset in range(coupling_rows.shape[1]):
        hit = (offsets == offset) & (offset < block_length[:, None])
        matrix = jnp.where(hit, coupling_rows[:, offset : offset + 1], matrix)
    return matrix


def shards(coeffs, projectors, block_coupling, atom_counts, wave_counts):
    moved_bands = lax.all_to_all(coeffs, "ga", split_axis=2, concat_axis=1, tiled=True)
    own_bands = coeffs.shape[1]
    group_bands = moved_bands.shape[1]
    wave_slots = projectors.shape[2]
    proj_total_rows = projectors.shape[0]
    in_sphere = (lax.iota(jnp.int32, wave_slots) < wave_counts[0]).astype(jnp.float32)
    masked = moved_bands * in_sphere.astype(jnp.bfloat16)
    real_part = masked[0]
    imag_part = masked[1]
    stacked = jnp.concatenate(
        [jnp.concatenate([real_part, imag_part], 1), jnp.concatenate([imag_part, -real_part], 1)], 0
    )
    flat_beta = projectors.reshape(proj_total_rows, 2 * wave_slots)
    contract_last = (((1,), (1,)), ((), ()))
    contract_first = (((0,), (0,)), ((), ()))
    ga_index = lax.axis_index("ga")
    local_terms = lax.dot_general(
        flat_beta, stacked, contract_last, preferred_element_type=jnp.float32
    )
    projections = lax.psum(local_terms, "ga")
    block_first, block_length = block_tables(atom_counts, lax.iota(jnp.int32, proj_total_rows))
    matrix = coupling_matrix(block_first, block_length, block_coupling, proj_total_rows)
    coupled = jnp.dot(
        matrix, projections, precision=lax.Precision.HIGHEST, preferred_element_type=jnp.float32
    )
    energy_terms = jnp.sum(projections * coupled, axis=0)
    group_energy = (energy_terms[:group_bands] + energy_terms[group_bands:]) / proj_total_rows
    band_energy = lax.dynamic_slice_in_dim(group_energy, ga_index * own_bands, own_bands, 0)
    total_energy = lax.psum(jnp.sum(group_energy), "band")
    products = lax.dot_general(
        coupled.astype(jnp.bfloat16), flat_beta, contract_first, preferred_element_type=jnp.float32
    )
    band_total = own_bands * lax.axis_size("ga") * lax.axis_size("band")
    total_energy = total_energy / math.sqrt(band_total)
    real_out = products[:group_bands, :wave_slots] - products[group_bands:, wave_slots:]
    imag_out = products[:group_bands, wave_slots:] + products[group_bands:, :wave_slots]
    result = (jnp.stack([real_out, imag_out]) * in_sphere).astype(jnp.bfloat16)
    applied = lax.all_to_all(result, "ga", split_axis=1, concat_axis=2, tiled=True)
    return (applied, band_energy, total_energy)


def solution(mesh):
    placed = (P(None, ("ga", "band"), None), P(None, None, "ga"), P(), P(), P("ga"))
    return jax.shard_map(
        shards,
        mesh=mesh,
        in_specs=placed,
        out_specs=(P(None, ("ga", "band"), None), P(("ga", "band")), P()),
        check_vma=False,
    )
```

profile of v0, /device:TPU:0, one launch (start us, length us, event | category | flops | bytes accessed | tf_op | source)
XLA Modules:
  0.0 439.4 jit_solution(13984395675737779399)
XLA Ops:
  7.2 38.0 %copy.21 = bf16[2,16,40960]{1,0,2:T(2,128)(2,1)} copy(bf16[2,16,40960]{2,1,0:T(8,128)(2,1)} %param.5) | data formatting | bytes 5242880 | tf_op args[0]
  45.1 24.1 %reshape.129 = bf16[8,2,81920]{2,1,0:T(2,128)(2,1)} reshape(bf16[40960,2,16]{2,1,0:T(2,128)(2,1)} %bitcast.40) | data formatting | bytes 5242880
  69.2 7.3 %all-to-all-start = ((bf16[8,2,81920]{2,1,0:T(2,128)(2,1)}), bf16[8,2,81920]{2,1,0:T(2,128)(2,1)S(1)}, u32[]{:S(2)}, u32[]{:S(2)}) async-start(bf16[8,2,81920]{2,1,0:T(2,128)(2,1)} %reshape.129), calls=%async_computation | async-start | bytes 5242880 | tf_op jit(solution)/shard_map/all_to_all | solution.py:28
  76.5 0.4 all-reduce.3.cloned.1.call-start
  77.6 23.8 %copy.29 = bf16[160,8,2,5120]{3,1,2,0:T(8,128)(2,1)} copy(bf16[160,8,2,5120]{3,2,1,0:T(2,128)(2,1)} %bitcast.41) | data formatting | bytes 52428800
  101.3 34.6 %all-to-all-done = bf16[8,2,81920]{2,1,0:T(2,128)(2,1)S(1)} async-done(((bf16[8,2,81920]{2,1,0:T(2,128)(2,1)}), bf16[8,2,81920]{2,1,0:T(2,128)(2,1)S(1)}, u32[]{:S(2)}, u32[]{:S(2)}) %all-to-all-start) | async-done | bytes 2621472 | tf_op jit(solution)/shard_map/all_to_all | solution.py:28
  136.0 17.1 %reshape.130 = bf16[40960,2,16]{2,1,0:T(2,128)(2,1)} reshape(bf16[8,2,81920]{2,1,0:T(2,128)(2,1)S(1)} %all-to-all-done) | data formatting | bytes 5242880
  153.0 37.5 %copy.28 = bf16[2,16,8,5120]{3,1,2,0:T(8,128)(2,1)S(1)} copy(bf16[2,16,8,5120]{1,0,3,2:T(2,128)(2,1)} %bitcast.39) | data formatting | bytes 5242880 | tf_op jit(solution)/shard_map/all_to_all | solution.py:28
  191.2 28.8 %fusion.138 = f32[1280,256]{0,1:T(8,128)} fusion(bf16[1280,10240]{1,0:T(8,128)(2,1)} %bitcast.37, bf16[128,5120]{1,0:T(8,128)(2,1)S(1)} %fusion.168, bf16[128,5120]{1,0:T(8,128)(2,1)S(1)} %get-tuple-element.28, bf16[128,5120]{1,0:T(8,128)(2,1)S(1)} %get-tuple-element.27), kind=kOutput, calls=%fused_computation.122 | convolution fusion | flops 6731857920 | bytes 31457280 | tf_op jit(solution)/shard_map/dot_general | solution.py:44
  221.3 81.6 %all-reduce.3.cloned.1.call-done = f32[1280,256]{0,1:T(8,128)} async-done(((f32[1280,256]{0,1:T(8,128)}), f32[1280,256]{0,1:T(8,128)}) %all-reduce.3.cloned.1.call-update) | async-done | bytes 1310736 | tf_op jit(solution)/shard_map/psum | solution.py:47
  303.0 39.1 %fusion = f32[1280,256]{1,0:T(8,128)} fusion(f32[1280,256]{0,1:T(8,128)} %all-reduce.3.cloned.1.call-done, f32[1280]{0:T(1024)S(1)} %get-tuple-element.19, f32[1280]{0:T(1024)S(1)} %get-tuple-element.20, f32[1280]{0:T(1024)S(1)} %get-tuple-element.4, f32[1280]{0:T(1024)S(1)} %get-tuple-element.5, f32[1280]{0:T(1024)S(1)} %get-tuple-element.6, ...), kind=kOutput, calls=%fused_computation | convolution fusion | flops 5123276800 | bytes 2741760 | tf_op jit(solution)/shard_map/dot_general | solution.py:50
  342.1 13.0 %fusion.144 = f32[256,10240]{1,0:T(8,128)S(1)} fusion(bf16[1280,10240]{1,0:T(8,128)(2,1)} %bitcast.38, f32[1280,256]{1,0:T(8,128)} %fusion), kind=kOutput, calls=%fused_computation.136 | convolution fusion | flops 6711214080 | bytes 38010880 | tf_op jit(solution)/shard_map/dot_general | solution.py:57
  355.1 0.8 fusion.142
  355.9 0.5 fusion.81
  356.4 4.2 copy.24
  360.6 3.7 all-to-all-start.1
  364.2 2.8 copy.26
  367.0 1.9 multiply_reduce_fusion
  368.9 0.6 fusion.169
  369.5 7.3 %psum.15 = f32[]{:T(128)} all-reduce(f32[]{:T(128)} %get-tuple-element.23), channel_id=1, replica_groups=mesh['ga'=8,'band'=4] {'band'}, use_global_device_ids=true, to_apply=%region_7.8 | all-reduce | flops 1 | bytes 8 | tf_op jit(solution)/shard_map/psum | solution.py:56
  376.9 0.6 dynamic_slice.3
  378.1 45.7 %all-to-all-done.1 = bf16[2,128,5120]{2,0,1:T(2,128)(2,1)S(1)} async-done(((bf16[2,128,5120]{2,0,1:T(2,128)(2,1)}), bf16[2,128,5120]{2,0,1:T(2,128)(2,1)S(1)}, u32[]{:S(2)}, u32[]{:S(2)}) %all-to-all-start.1) | async-done | bytes 2621472 | tf_op jit(solution)/shard_map/all_to_all | solution.py:65
  423.8 2.9 copy.25
  426.7 4.5 %all_to_all.33 = bf16[2,16,40960]{2,1,0:T(8,128)(2,1)} reshape(bf16[2,16,8,5120]{3,2,1,0:T(8,128)(2,1)} %copy.25) | data formatting | bytes 5242880 | tf_op jit(solution)/shard_map/all_to_all | solution.py:65
  (19 shorter events, 1.9 us)
Async XLA Ops:
  69.2 66.8 %all-to-all-start = ((bf16[8,2,81920]{2,1,0:T(2,128)(2,1)}), bf16[8,2,81920]{2,1,0:T(2,128)(2,1)S(1)}, u32[]{:S(2)}, u32[]{:S(2)}) async-start(bf16[8,2,81920]{2,1,0:T(2,128)(2,1)} %reshape.129), calls=%async_computation | async-start | bytes 5242880 | tf_op jit(solution)/shard_map/all_to_all | solution.py:28
  76.5 226.5 %all-reduce.3.cloned.1.call-start = ((), (), s32[]{:S(2)}) async-start(), calls=%async_computation.2 | async-start | bytes 2621440 | tf_op jit(solution)/shard_map/psum | solution.py:47
  191.2 28.9 %copy-start.1 = (s32[160]{0:T(256)S(1)}, s32[160]{0:T(256)}, u32[]{:S(2)}) copy-start(s32[160]{0:T(256)} %param.8) | copy-start | bytes 1924
  191.2 29.4 %copy-start = (f32[1280,18]{0,1:T(8,128)S(1)}, f32[1280,18]{0,1:T(8,128)}, u32[]{:S(2)}) copy-start(f32[1280,18]{0,1:T(8,128)} %param.7) | copy-start | bytes 276484
  360.6 63.2 %all-to-all-start.1 = ((bf16[2,128,5120]{2,0,1:T(2,128)(2,1)}), bf16[2,128,5120]{2,0,1:T(2,128)(2,1)S(1)}, u32[]{:S(2)}, u32[]{:S(2)}) async-start(bf16[2,128,5120]{2,0,1:T(2,128)(2,1)} %copy.24), calls=%async_computation.1 | async-start | bytes 5242880 | tf_op jit(solution)/shard_map/all_to_all | solution.py:65
Sparse Core Ops, SparseCore 0:
  220.2 82.7 all-reduce.2
where the time goes:
time: 447 us; the launch traced here: 439 us
  waiting for transfers between devices  162 us (36%)
  local copies, waits for them, and re-layouts  156 us (35%)
  matrix products  81 us (18%)
  between operations  16.8 us (4%)
  starting transfers between devices  11.4 us (3%)
  blocking collectives  7.33 us (2%)
  other arithmetic  4.94 us (1%)
    unnamed x8, local copies, waits for them, and re-layouts  103 us
    psum x1, waiting for transfers between devices, shards(): projections = lax.psum(local_terms, 'ga')  81.6 us
    all_to_all x1, waiting for transfers between devices, shards(): lax.all_to_all(result, 'ga', split_axis=1, concat_axis=2, tiled=True)  45.7 us
    dot_general x1, matrix products, shards(): jnp.dot(matrix, projections, precision=lax.Precision.HIGHEST, preferred_e...  39.1 us
    all_to_all x1, local copies, waits for them, and re-layouts, shards(): lax.all_to_all(coeffs, 'ga', split_axis=2, concat_axis=1, tiled=True)  37.5 us
    all_to_all x1, waiting for transfers between devices, shards(): lax.all_to_all(coeffs, 'ga', split_axis=2, concat_axis=1, tiled=True)  34.6 us
    dot_general x1, matrix products, shards(): lax.dot_general(flat_beta, stacked, contract_last, preferred_element_type...  28.8 us
    dot_general x1, matrix products, shards(): lax.dot_general(coupled.astype(jnp.bfloat16), flat_beta, contract_first,...  13 us
  transfers between devices with their start and end apart: 3, of which 3 were waited for; matrix products, arithmetic and copies ran while one was open for 7% of the time, Pallas kernels for 0%

commit v1 on v0

--- a/solution.py
+++ b/solution.py
@@ -44,7 +44,11 @@
     local_terms = lax.dot_general(
         flat_beta, stacked, contract_last, preferred_element_type=jnp.float32
     )
-    projections = lax.psum(local_terms, "ga")
+
+    def slot_wrap(dev_axis, page):
+        return jnp.sum(jax.lax.all_gather(page, axis_name=dev_axis), axis=0)
+
+    projections = slot_wrap("ga", local_terms)
     block_first, block_length = block_tables(atom_counts, lax.iota(jnp.int32, proj_total_rows))
     matrix = coupling_matrix(block_first, block_length, block_coupling, proj_total_rows)
     coupled = jnp.dot(

time: 447 us -> 515 us (1.15)
  waiting for transfers between devices: 162 us -> 234 us
  matrix products: 81 us -> 70.1 us
  local copies, waits for them, and re-layouts: 156 us -> 163 us
    all_gather x0 -> x1, waiting for transfers between devices: none -> 148 us  [slot_wrap(): return jnp.sum(jax.lax.all_gather(page, axis_name=dev_axis), axis=0)]
    psum x1 -> x0, waiting for transfers between devices: 81.6 us -> none  [shards(): projections = lax.psum(local_terms, 'ga')]
    dot_general x1, matrix products: 39.1 us -> 28.7 us  [shards(): jnp.dot(matrix, projections, precision=lax.Precision.HIGHEST, preferred_e...]
    unnamed x8 -> x9, local copies, waits for them, and re-layouts: 103 us -> 111 us
  transfers between devices with their start and end apart: 3 -> 3, of which waited for: 3 -> 3; matrix products, arithmetic and copies ran while one was open for 7% -> 5% of each run, Pallas kernels for 0% -> 0%
where the time goes in v1:
time: 515 us; the launch traced here: 507 us
  waiting for transfers between devices  234 us (45%)
  local copies, waits for them, and re-layouts  163 us (32%)
  matrix products  70.1 us (14%)
  between operations  16.8 us (3%)
  starting transfers between devices  11.2 us (2%)
  blocking collectives  6.75 us (1%)
  other arithmetic  5.33 us (1%)
    all_gather x1, waiting for transfers between devices, slot_wrap(): return jnp.sum(jax.lax.all_gather(page, axis_name=dev_axis), axis=0)  148 us
    unnamed x9, local copies, waits for them, and re-layouts  111 us
    all_to_all x1, waiting for transfers between devices, shards(): lax.all_to_all(result, 'ga', split_axis=1, concat_axis=2, tiled=True)  50.4 us
    all_to_all x1, local copies, waits for them, and re-layouts, shards(): lax.all_to_all(coeffs, 'ga', split_axis=2, concat_axis=1, tiled=True)  37.5 us
    all_to_all x1, waiting for transfers between devices, shards(): lax.all_to_all(coeffs, 'ga', split_axis=2, concat_axis=1, tiled=True)  34.7 us
    dot_general x1, matrix products, shards(): lax.dot_general(flat_beta, stacked, contract_last, preferred_element_type...  29.3 us
    dot_general x1, matrix products, shards(): jnp.dot(matrix, projections, precision=lax.Precision.HIGHEST, preferred_e...  28.7 us
    dot_general x1, matrix products, shards(): lax.dot_general(coupled.astype(jnp.bfloat16), flat_beta, contract_first,...  12.1 us
  transfers between devices with their start and end apart: 3, of which 3 were waited for; matrix products, arithmetic and copies ran while one was open for 5% of the time, Pallas kernels for 0%

profile of v1, /device:TPU:0, one launch (start us, length us, event | category | flops | bytes accessed | tf_op | source)
XLA Modules:
  0.0 506.9 jit_solution(8275240517535720569)
XLA Ops:
  7.2 38.0 %copy.18 = bf16[2,16,40960]{1,0,2:T(2,128)(2,1)} copy(bf16[2,16,40960]{2,1,0:T(8,128)(2,1)} %param.5) | data formatting | bytes 5242880 | tf_op args[0]
  45.1 24.1 %reshape.130 = bf16[8,2,81920]{2,1,0:T(2,128)(2,1)} reshape(bf16[40960,2,16]{2,1,0:T(2,128)(2,1)} %bitcast.46) | data formatting | bytes 5242880
  69.2 7.3 %all-to-all-start = ((bf16[8,2,81920]{2,1,0:T(2,128)(2,1)}), bf16[8,2,81920]{2,1,0:T(2,128)(2,1)S(1)}, u32[]{:S(2)}, u32[]{:S(2)}) async-start(bf16[8,2,81920]{2,1,0:T(2,128)(2,1)} %reshape.130), calls=%async_computation | async-start | bytes 5242880 | tf_op jit(solution)/shard_map/all_to_all | solution.py:28
  77.5 23.8 %copy.26 = bf16[160,8,2,5120]{3,1,2,0:T(8,128)(2,1)} copy(bf16[160,8,2,5120]{3,2,1,0:T(2,128)(2,1)} %bitcast.47) | data formatting | bytes 52428800
  101.3 34.7 %all-to-all-done = bf16[8,2,81920]{2,1,0:T(2,128)(2,1)S(1)} async-done(((bf16[8,2,81920]{2,1,0:T(2,128)(2,1)}), bf16[8,2,81920]{2,1,0:T(2,128)(2,1)S(1)}, u32[]{:S(2)}, u32[]{:S(2)}) %all-to-all-start) | async-done | bytes 2621472 | tf_op jit(solution)/shard_map/all_to_all | solution.py:28
  136.0 17.1 %reshape.131 = bf16[40960,2,16]{2,1,0:T(2,128)(2,1)} reshape(bf16[8,2,81920]{2,1,0:T(2,128)(2,1)S(1)} %all-to-all-done) | data formatting | bytes 5242880
  153.0 37.5 %copy.25 = bf16[2,16,8,5120]{3,1,2,0:T(8,128)(2,1)S(1)} copy(bf16[2,16,8,5120]{1,0,3,2:T(2,128)(2,1)} %bitcast.45) | data formatting | bytes 5242880 | tf_op jit(solution)/shard_map/all_to_all | solution.py:28
  191.2 29.3 %fusion.138 = f32[1280,256]{0,1:T(8,128)} fusion(bf16[1280,10240]{1,0:T(8,128)(2,1)} %bitcast.43, bf16[128,5120]{1,0:T(8,128)(2,1)S(1)} %fusion.168, bf16[128,5120]{1,0:T(8,128)(2,1)S(1)} %get-tuple-element.28, bf16[128,5120]{1,0:T(8,128)(2,1)S(1)} %get-tuple-element.27), kind=kOutput, calls=%fused_computation.123 | convolution fusion | flops 6731857920 | bytes 31457280 | tf_op jit(solution)/shard_map/dot_general | solution.py:44
  221.8 148.5 %all-gather.3.cloned.1.call-done = f32[10240,256]{0,1:T(8,128)} async-done(((f32[1280,256]{0,1:T(8,128)}), f32[10240,256]{0,1:T(8,128)}) %all-gather.3.cloned.1.call-update) | async-done | bytes 10485776 | tf_op jit(solution)/shard_map/all_gather | solution.py:49
  370.3 8.3 %copy.27 = f32[32,8,8,1280]{3,2,1,0:T(8,128)S(1)} copy(f32[32,8,8,1280]{3,1,2,0:T(8,128)} %bitcast.48) | data formatting | bytes 20971520
  378.6 2.5 bitcast_reduce_fusion
  381.1 1.5 copy.23
  382.5 28.7 %multiply_reduce_fusion = (f32[256]{0:T(256)S(1)}, bf16[1280,256]{1,0:T(8,128)(2,1)S(1)}) fusion(f32[1280,256]{1,0:T(8,128)} %copy.23, f32[1280,256]{0,1:T(8,128)S(1)} %bitcast_reduce_fusion, f32[1280]{0:T(1024)S(1)} %get-tuple-element.19, f32[1280]{0:T(1024)S(1)} %get-tuple-element.20, f32[1280]{0:T(1024)S(1)} %get-tuple-element.4, ...), kind=kOutput, calls=%fused_computation.131 | convolution fusion | flops 5124259840 | bytes 3398144 | tf_op jit(solution)/shard_map/dot_general | solution.py:54
  411.2 12.1 %fusion.144 = f32[256,10240]{1,0:T(8,128)S(1)} fusion(bf16[1280,10240]{1,0:T(8,128)(2,1)} %bitcast.44, bf16[1280,256]{1,0:T(8,128)(2,1)S(1)} %get-tuple-element.50), kind=kOutput, calls=%fused_computation.137 | convolution fusion | flops 6710886400 | bytes 37355520 | tf_op jit(solution)/shard_map/dot_general | solution.py:61
  423.4 0.6 fusion.142
  424.0 0.5 fusion.81
  424.4 4.2 copy.21
  428.6 3.6 all-to-all-start.1
  432.3 0.6 fusion.169
  432.9 6.7 %psum.7 = f32[]{:T(128)} all-reduce(f32[]{:T(128)} %get-tuple-element.23), channel_id=1, replica_groups=mesh['ga'=8,'band'=4] {'band'}, use_global_device_ids=true, to_apply=%region_7.8 | all-reduce | flops 1 | bytes 8 | tf_op jit(solution)/shard_map/psum | solution.py:60
  439.6 0.6 dynamic_slice.3
  440.8 50.4 %all-to-all-done.1 = bf16[2,128,5120]{2,0,1:T(2,128)(2,1)S(1)} async-done(((bf16[2,128,5120]{2,0,1:T(2,128)(2,1)}), bf16[2,128,5120]{2,0,1:T(2,128)(2,1)S(1)}, u32[]{:S(2)}, u32[]{:S(2)}) %all-to-all-start.1) | async-done | bytes 2621472 | tf_op jit(solution)/shard_map/all_to_all | solution.py:69
  491.2 2.9 copy.22
  494.2 4.5 all_to_all.33
  (20 shorter events, 2.2 us)
Async XLA Ops:
  69.2 66.8 %all-to-all-start = ((bf16[8,2,81920]{2,1,0:T(2,128)(2,1)}), bf16[8,2,81920]{2,1,0:T(2,128)(2,1)S(1)}, u32[]{:S(2)}, u32[]{:S(2)}) async-start(bf16[8,2,81920]{2,1,0:T(2,128)(2,1)} %reshape.130), calls=%async_computation | async-start | bytes 5242880 | tf_op jit(solution)/shard_map/all_to_all | solution.py:28
  76.5 293.8 %all-gather.3.cloned.1.call-start = ((), (), s32[]{:S(2)}) async-start(), calls=%async_computation.2 | async-start | bytes 11796480 | tf_op jit(solution)/shard_map/all_gather | solution.py:49
  191.2 29.4 %copy-start.1 = (s32[160]{0:T(256)S(1)}, s32[160]{0:T(256)}, u32[]{:S(2)}) copy-start(s32[160]{0:T(256)} %param.8) | copy-start | bytes 1924
  191.2 29.9 %copy-start = (f32[1280,18]{0,1:T(8,128)S(1)}, f32[1280,18]{0,1:T(8,128)}, u32[]{:S(2)}) copy-start(f32[1280,18]{0,1:T(8,128)} %param.7) | copy-start | bytes 276484
  428.6 62.6 %all-to-all-start.1 = ((bf16[2,128,5120]{2,0,1:T(2,128)(2,1)}), bf16[2,128,5120]{2,0,1:T(2,128)(2,1)S(1)}, u32[]{:S(2)}, u32[]{:S(2)}) async-start(bf16[2,128,5120]{2,0,1:T(2,128)(2,1)} %copy.21), calls=%async_computation.1 | async-start | bytes 5242880 | tf_op jit(solution)/shard_map/all_to_all | solution.py:69
Sparse Core Ops, SparseCore 0:
  220.7 149.5 all-gather.2
